TPU v7x, 512 devices: a whole 4x8x8 slice. The times are simulated.
512 devices in a mesh: ops: 64 (over y_lo, z, core), sec: 8 (over y_hi, x).
Axes of the slice: x: 4, y: 8 (y_hi: 2, y_lo: 4; y = y_hi * 4 + y_lo), z: 8, core: 2. Of those that a mesh axis runs over, the one named last changes fastest.
Arguments:
- wavefunction: bfloat16 [8, 512, 512], P('sec', 'ops'), may hold values from -6 to 6
- left_blocks: bfloat16 [8, 256, 512, 512], P('sec', 'ops'), may hold values from -0.25 to 0.25
- right_blocks: bfloat16 [8, 256, 512, 512], P('sec', 'ops'), may hold values from -0.03125 to 0.03125
- pair_index: int32 [8, 256], P('sec', 'ops'), may hold values from 0 to 3
- term_counts: int32 [8, 64], P('sec'), may hold values from 0 to 4, as said below
- charges: int32 [8], P('sec'), may hold values from 0 to 7
Outputs:
- applied: bfloat16 [8, 512, 512], P('sec', 'ops')
Inputs may be any that keep to these rules, and one draw needn't show every extreme that they name: `term_counts`: in every sector exactly one device row holds 4 live terms and every other holds 0 to 2; live terms fill a device's slots from slot 0 on.
All inputs are finite; a program needn't handle non-finite values.
Results may differ from a plain program's by a relative error of at most 0.0029.
Values may be sent and summed in bfloat16 or wider, within the bound.
No kernel may reach another device: no remote copies, remote signals or barrier semaphores. Data moves between devices by JAX's collectives and lax.ppermute only.
A program may use at most 64 MiB of HBM per device.

v0:
```python
import jax
import jax.numpy as jnp
from jax import lax
from jax.experimental import pallas as pl
from jax.experimental.pallas import tpu as pltpu
from jax.sharding import PartitionSpec as P


CORES = 2
TURNED_SECTOR = 3


def core_pairs(length):
    return [[chip * CORES + core for core in range(CORES)] for chip in range(length // CORES)]


def same_core(length):
    return [[chip * CORES + core for chip in range(length // CORES)] for core in range(CORES)]


def to_partner(x):
    return lax.ppermute(x, "ops", [(i, i ^ 1) for i in range(lax.axis_size("ops"))])


def fetch_kernel(counts_ref, picks_ref, lefts_ref, rights_ref, left_buf, right_buf, meta_ref,
                 left_sems, right_sems):
    position = lax.axis_index("ops")
    core = position % CORES
    live = counts_ref[0, position]
    slots = left_buf.shape[0]

    def copies(slot):
        return (
            pltpu.make_async_copy(
                lefts_ref.at[slot, :, core], left_buf.at[slot], left_sems.at[slot]
            ),
            pltpu.make_async_copy(
                rights_ref.at[0, picks_ref[0, slot]], right_buf.at[slot], right_sems.at[slot]
            ),
        )

    meta_ref[0] = live
    meta_ref[1] = counts_ref[0, position + 1 - 2 * core]
    for slot in range(slots):

        @pl.when(slot < live)
        def _():
            for copy in copies(slot):
                copy.start()

    for slot in range(slots):

        @pl.when(slot < live)
        def _():
            for copy in copies(slot):
                copy.wait()


def fetched_blocks(term_counts, pair_index, lefts, right_blocks):
    smem = pl.BlockSpec(memory_space=pltpu.SMEM)
    hbm = pl.BlockSpec(memory_space=pltpu.HBM)
    vmem = pl.BlockSpec(memory_space=pltpu.VMEM)
    slots, chips, _, band, size = lefts.shape
    return pl.pallas_call(
        fetch_kernel,
        out_shape=(
            pltpu.VMEM((slots, chips, band, size), jnp.bfloat16),
            pltpu.VMEM(right_blocks.shape[1:], jnp.bfloat16),
            pltpu.SMEM((CORES,), jnp.int32),
        ),
        in_specs=[smem, smem, hbm, hbm],
        out_specs=(vmem, vmem, smem),
        scratch_shapes=[pltpu.SemaphoreType.DMA((slots,)), pltpu.SemaphoreType.DMA((slots,))],
        compiler_params=pltpu.CompilerParams(vmem_limit_bytes=8 * 1024 * 1024),
        name="fetch",
    )(
        pltpu.with_memory_space_constraint(term_counts, pltpu.HBM),
        pltpu.with_memory_space_constraint(pair_index, pltpu.HBM),
        pltpu.with_memory_space_constraint(lefts, pltpu.HBM),
        pltpu.with_memory_space_constraint(right_blocks, pltpu.HBM),
    )


def terms_kernel(psi_ref, meta_ref, lefts_ref, rights_ref, partner_lefts_ref, partner_rights_ref,
                 sum_ref, left_buf, right_buf, psi_buf, acc_ref, left_sems, right_sems):
    core = lax.axis_index("ops") % CORES
    slots, chips, band, size = lefts_ref.shape
    rows = chips * band
    own_live, partner_live = meta_ref[0], meta_ref[1]

    def left_copy(slot):
        return pltpu.make_async_copy(
            partner_lefts_ref.at[slot, :, core], left_buf.at[slot], left_sems.at[slot]
        )

    def right_copy(slot):
        return pltpu.make_async_copy(
            partner_rights_ref.at[slot], right_buf.at[slot], right_sems.at[slot]
        )

    for slot in range(slots):

        @pl.when(slot < partner_live)
        def _():
            left_copy(slot).start()
            right_copy(slot).start()

    for chip in range(chips):
        for c in range(CORES):
            psi_buf[pl.ds((chip * CORES + c) * band, band), :] = psi_ref[c, chip]
    acc_ref[...] = jnp.zeros_like(acc_ref)

    def own_term(slot, carry):
        product = jnp.dot(
            lefts_ref[slot].reshape(rows, size), psi_buf[...], preferred_element_type=jnp.float32
        ).astype(jnp.bfloat16)
        acc_ref[...] += jnp.dot(product, rights_ref[slot], preferred_element_type=jnp.float32)
        return carry

    def partner_term(slot, carry):
        left_copy(slot).wait()
        product = jnp.dot(
            left_buf[slot].reshape(rows, size), psi_buf[...], preferred_element_type=jnp.float32
        ).astype(jnp.bfloat16)
        right_copy(slot).wait()
        acc_ref[...] += jnp.dot(product, right_buf[slot], preferred_element_type=jnp.float32)
        return carry

    lax.fori_loop(0, own_live, own_term, 0)
    lax.fori_loop(0, partner_live, partner_term, 0)
    turn = jnp.where(lax.axis_index("sec") == TURNED_SECTOR, chips // 2, 0)
    for chip in range(chips):
        sum_ref[lax.rem(chip + turn, chips)] = acc_ref[pl.ds(chip * band, band), :].astype(
            jnp.bfloat16
        )


def summed_terms(psi, meta, lefts, rights, partner_lefts, partner_rights):
    slots, chips, band, size = lefts.shape
    columns = psi.shape[-1]
    vmem = pl.BlockSpec(memory_space=pltpu.VMEM)
    smem = pl.BlockSpec(memory_space=pltpu.SMEM)
    hbm = pl.BlockSpec(memory_space=pltpu.HBM)
    return pl.pallas_call(
        terms_kernel,
        out_shape=jax.ShapeDtypeStruct((chips, band, columns), jnp.bfloat16),
        in_specs=[vmem, smem, vmem, vmem, hbm, hbm],
        out_specs=vmem,
        scratch_shapes=[
            pltpu.VMEM(lefts.shape, jnp.bfloat16),
            pltpu.VMEM(rights.shape, jnp.bfloat16),
            pltpu.VMEM((size, columns), jnp.bfloat16),
            pltpu.VMEM((chips * band, columns), jnp.float32),
            pltpu.SemaphoreType.DMA((slots,)),
            pltpu.SemaphoreType.DMA((slots,)),
        ],
        compiler_params=pltpu.CompilerParams(vmem_limit_bytes=24 * 1024 * 1024),
        name="terms",
    )(
        psi,
        meta,
        lefts,
        rights,
        pltpu.with_memory_space_constraint(partner_lefts, pltpu.HBM),
        pltpu.with_memory_space_constraint(partner_rights, pltpu.HBM),
    )


def shift_pairs(length, sectors):
    pairs = []
    for position in range(length):
        for sector in range(sectors - 1):
            turned = (position + length // 2) % length if sector == TURNED_SECTOR else position
            pairs.append((turned * sectors + sector, position * sectors + sector + 1))
    return pairs


def per_device(wavefunction, left_blocks, right_blocks, pair_index, term_counts, charges):
    own_rows = wavefunction[0]
    length, sectors = lax.axis_size("ops"), lax.axis_size("sec")
    chips = length // CORES
    pairs, peers = core_pairs(length), same_core(length)

    copies = jnp.broadcast_to(own_rows[None], (chips, *own_rows.shape))
    bands = lax.all_to_all(copies, "ops", 0, 0, axis_index_groups=peers, tiled=True)

    by_band = (left_blocks.shape[1], chips, CORES, own_rows.shape[0], left_blocks.shape[3])
    lefts, rights, meta = fetched_blocks(
        term_counts, pair_index, left_blocks.reshape(by_band), right_blocks
    )
    partner_lefts = to_partner(left_blocks).reshape(by_band)
    partner_rights = to_partner(rights)

    psi = lax.all_gather(bands, "ops", axis_index_groups=pairs)
    chip_sum = summed_terms(psi, meta, lefts, rights, partner_lefts, partner_rights)
    parts = lax.all_to_all(chip_sum, "ops", 0, 0, axis_index_groups=peers, tiled=True)
    summed = parts.astype(jnp.float32).sum(axis=0)

    raised = lax.ppermute(summed, ("ops", "sec"), shift_pairs(length, sectors))
    onsite = 0.5 * charges[0].astype(jnp.float32) * own_rows.astype(jnp.float32)
    return (onsite + raised).astype(jnp.bfloat16)[None]


def solution(mesh):
    return jax.shard_map(
        per_device,
        mesh=mesh,
        in_specs=(
            P("sec", "ops", None),
            P("sec", "ops", None, None),
            P("sec", "ops", None, None),
            P("sec", "ops"),
            P("sec", None),
            P("sec"),
        ),
        out_specs=P("sec", "ops", None),
        check_vma=False,
    )
```

profile of v0, /device:TPU:56, one launch (start us, length us, event | category | flops | bytes accessed | tf_op | source)
XLA Modules:
  0.0 64.9 jit_solution(10980268868648152749)
XLA Ops:
  0.0 0.0 copy-start
  0.0 0.0 copy-start.3
  0.0 0.9 %fetch.1 = (bf16[4,32,8,512]{3,2,1,0:T(8,128)(2,1)S(1)}, bf16[4,512,512]{2,1,0:T(8,128)(2,1)S(1)}, s32[2]{0:T(128)S(4)}) custom-call(s32[1,64]{1,0:T(1,128)} %counts_ref.1, s32[1,4]{1,0:T(1,128)} %picks_ref.1, bf16[4,32,2,8,512]{4,3,2,1,0:T(8,128)(2,1)} %bitcast.9, bf16[1,4,512,512]{3,2,1,0:T(8,128)(2,1)} %rights_ref.1), custom_call_target="tpu_custom_call" | custom-call | tf_op jit(solution)/shard_map/fetch/pallas_call | solution.py:64
  0.9 1.9 %collective-permute-start.1 = (bf16[4,512,512]{2,1,0:T(8,128)(2,1)S(1)}, bf16[4,512,512]{2,1,0:T(8,128)(2,1)S(1)}, u32[]{:S(2)}, u32[]{:S(2)}) collective-permute-start(bf16[4,512,512]{2,1,0:T(8,128)(2,1)S(1)} %get-tuple-element.10.rights_ref), channel_id=1, source_target_pairs={{0,8},{8,0},{16,24},{24,16},{32,40},{40,32},{48,56},{56,48},{64,72... | collective-permute-start | bytes 6291464 | tf_op jit(solution)/shard_map/ppermute | solution.py:22
  2.9 0.0 copy-done
  2.9 2.4 %collective-permute-start = (bf16[1,4,512,512]{3,2,1,0:T(8,128)(2,1)S(1)}, bf16[1,4,512,512]{3,2,1,0:T(8,128)(2,1)S(1)}, u32[]{:S(2)}, u32[]{:S(2)}) collective-permute-start(bf16[1,4,512,512]{3,2,1,0:T(8,128)(2,1)S(1)} %copy-done), channel_id=1, source_target_pairs={{0,8},{8,0},{16,24},{24,16},{32,40},{40,32},{48,56},{56,48},{64,72... | collective-permute-start | bytes 6291464 | tf_op jit(solution)/shard_map/ppermute | solution.py:22
  5.3 0.0 copy-done.3
  5.3 25.7 %all_to_all.10 = bf16[32,8,512]{2,1,0:T(8,128)(2,1)S(1)} all-to-all(bf16[32,8,512]{2,1,0:T(8,128)(2,1)S(1)} %broadcast_in_dim.8), channel_id=1, replica_groups={{0,16,32,48,64,80,96,112,128,144,160,176,192,208,224,240,256,272,288,30..., dimensions={0} | all-to-all | bytes 524288 | tf_op jit(solution)/shard_map/all_to_all | solution.py:185
  31.0 2.2 %all-gather = bf16[64,8,512]{2,1,0:T(8,128)(2,1)S(1)} all-gather(bf16[32,8,512]{2,1,0:T(8,128)(2,1)S(1)} %all_to_all.10), channel_id=2, replica_groups={{0,8},{16,24},{32,40},{48,56},{64,72},{80,88},{96,104},{112,120},{128,1..., dimensions={0}, use_global_device_ids=true | all-gather | bytes 786432 | tf_op jit(solution)/shard_map/all_gather | solution.py:194
  33.2 0.0 collective-permute-done.1.partner_rights_ref
  33.2 0.0 copy-start.1
  33.2 0.0 collective-permute-done
  33.2 0.0 copy-start.2
  33.2 1.3 %copy-done.1 = bf16[4,512,512]{2,1,0:T(8,128)(2,1)} copy-done((bf16[4,512,512]{2,1,0:T(8,128)(2,1)}, bf16[4,512,512]{2,1,0:T(8,128)(2,1)S(1)}, u32[]{:S(2)}) %copy-start.1) | copy-done | bytes 2097176
  34.5 0.7 %copy-done.2 = bf16[1,4,512,512]{3,2,1,0:T(8,128)(2,1)} copy-done((bf16[1,4,512,512]{3,2,1,0:T(8,128)(2,1)}, bf16[1,4,512,512]{3,2,1,0:T(8,128)(2,1)S(1)}, u32[]{:S(2)}) %copy-start.2) | copy-done | bytes 2097176
  35.2 0.2 terms.1
  35.4 19.0 %all_to_all.11 = bf16[32,8,512]{2,1,0:T(8,128)(2,1)S(1)} all-to-all(bf16[32,8,512]{2,1,0:T(8,128)(2,1)S(1)} %terms.1), channel_id=1, replica_groups={{0,16,32,48,64,80,96,112,128,144,160,176,192,208,224,240,256,272,288,30..., dimensions={0} | all-to-all | bytes 524288 | tf_op jit(solution)/shard_map/all_to_all | solution.py:196
  54.4 4.1 %collective-permute-start.2 = (f32[8,512]{1,0:T(8,128)S(1)}, f32[8,512]{1,0:T(8,128)S(1)}, u32[]{:S(2)}, u32[]{:S(2)}) collective-permute-start(f32[8,512]{1,0:T(8,128)S(1)} %convert_reduce_fusion), channel_id=1, source_target_pairs={{0,1},{1,2},{2,3},{259,4},{4,5},{5,6},{6,7},{8,9},{9,10},{10,11},{... | collective-permute-start | bytes 49160 | tf_op jit(solution)/shard_map/ppermute | solution.py:199
  59.2 5.1 %collective-permute-done.2 = f32[8,512]{1,0:T(8,128)S(1)} collective-permute-done((f32[8,512]{1,0:T(8,128)S(1)}, f32[8,512]{1,0:T(8,128)S(1)}, u32[]{:S(2)}, u32[]{:S(2)}) %collective-permute-start.2) | collective-permute-done | bytes 16416 | tf_op jit(solution)/shard_map/ppermute | solution.py:199
  64.3 0.6 fusion
  (2 shorter events, 0.1 us)
Async XLA Ops:
  0.0 2.9 %copy-start = (bf16[1,4,512,512]{3,2,1,0:T(8,128)(2,1)S(1)}, bf16[1,4,512,512]{3,2,1,0:T(8,128)(2,1)}, u32[]{:S(2)}) copy-start(bf16[1,4,512,512]{3,2,1,0:T(8,128)(2,1)} %param.7) | copy-start | bytes 6291460
  0.0 5.3 %copy-start.3 = (bf16[1,8,512]{2,1,0:T(8,128)(2,1)S(1)}, bf16[1,8,512]{2,1,0:T(8,128)(2,1)}, u32[]{:S(2)}) copy-start(bf16[1,8,512]{2,1,0:T(8,128)(2,1)} %param.6) | copy-start | bytes 24580
  0.9 32.3 %collective-permute-start.1 = (bf16[4,512,512]{2,1,0:T(8,128)(2,1)S(1)}, bf16[4,512,512]{2,1,0:T(8,128)(2,1)S(1)}, u32[]{:S(2)}, u32[]{:S(2)}) collective-permute-start(bf16[4,512,512]{2,1,0:T(8,128)(2,1)S(1)} %get-tuple-element.10.rights_ref), channel_id=1, source_target_pairs={{0,8},{8,0},{16,24},{24,16},{32,40},{40,32},{48,56},{56,48},{64,72... | collective-permute-start | bytes 6291464 | tf_op jit(solution)/shard_map/ppermute | solution.py:22
  2.9 30.4 %collective-permute-start = (bf16[1,4,512,512]{3,2,1,0:T(8,128)(2,1)S(1)}, bf16[1,4,512,512]{3,2,1,0:T(8,128)(2,1)S(1)}, u32[]{:S(2)}, u32[]{:S(2)}) collective-permute-start(bf16[1,4,512,512]{3,2,1,0:T(8,128)(2,1)S(1)} %copy-done), channel_id=1, source_target_pairs={{0,8},{8,0},{16,24},{24,16},{32,40},{40,32},{48,56},{56,48},{64,72... | collective-permute-start | bytes 6291464 | tf_op jit(solution)/shard_map/ppermute | solution.py:22
  33.2 1.3 %copy-start.1 = (bf16[4,512,512]{2,1,0:T(8,128)(2,1)}, bf16[4,512,512]{2,1,0:T(8,128)(2,1)S(1)}, u32[]{:S(2)}) copy-start(bf16[4,512,512]{2,1,0:T(8,128)(2,1)S(1)} %collective-permute-done.1.partner_rights_ref) | copy-start | bytes 6291460
  33.2 2.0 %copy-start.2 = (bf16[1,4,512,512]{3,2,1,0:T(8,128)(2,1)}, bf16[1,4,512,512]{3,2,1,0:T(8,128)(2,1)S(1)}, u32[]{:S(2)}) copy-start(bf16[1,4,512,512]{3,2,1,0:T(8,128)(2,1)S(1)} %collective-permute-done) | copy-start | bytes 6291460
  54.4 9.9 %collective-permute-start.2 = (f32[8,512]{1,0:T(8,128)S(1)}, f32[8,512]{1,0:T(8,128)S(1)}, u32[]{:S(2)}, u32[]{:S(2)}) collective-permute-start(f32[8,512]{1,0:T(8,128)S(1)} %convert_reduce_fusion), channel_id=1, source_target_pairs={{0,1},{1,2},{2,3},{259,4},{4,5},{5,6},{6,7},{8,9},{9,10},{10,11},{... | collective-permute-start | bytes 49160 | tf_op jit(solution)/shard_map/ppermute | solution.py:199
where the time goes:
time: 65.2 us; the launch traced here: 64.9 us
  blocking collectives  46.9 us (72%)
  starting transfers between devices  8.43 us (13%)
  waiting for transfers between devices  5.1 us (8%)
  local copies, waits for them, and re-layouts  1.98 us (3%)
  Pallas kernels  1.1 us (2%)
  between operations  0.73 us (1%)
    all_to_all x1, blocking collectives, per_device(): lax.all_to_all(copies, 'ops', 0, 0, axis_index_groups=peers, tiled=True)  25.7 us
    all_to_all x1, blocking collectives, per_device(): lax.all_to_all(chip_sum, 'ops', 0, 0, axis_index_groups=peers, tiled=True)  19 us
    ppermute x1, waiting for transfers between devices, per_device(): raised = lax.ppermute(summed, ('ops', 'sec'), shift_pairs(length, sectors))  5.09 us
    ppermute x2, starting transfers between devices, to_partner(): lax.ppermute(x, 'ops', [(i, i ^ 1) for i in range(lax.axis_size('ops'))])  4.33 us
    ppermute x1, starting transfers between devices, per_device(): raised = lax.ppermute(summed, ('ops', 'sec'), shift_pairs(length, sectors))  4.1 us
    all_gather x1, blocking collectives, per_device(): psi = lax.all_gather(bands, 'ops', axis_index_groups=pairs)  2.17 us
    unnamed x8, local copies, waits for them, and re-layouts  1.96 us
  transfers between devices with their start and end apart: 3, of which 1 were waited for; matrix products, arithmetic and copies ran while one was open for 0% of the time, Pallas kernels for 0%

commit v1 on v0

--- a/solution.py
+++ b/solution.py
@@ -10,12 +10,22 @@
 TURNED_SECTOR = 3
 
 
+GATHER_ORDER = (
+    31, 30, 29, 28, 27, 26, 25, 24, 23, 22, 21, 20, 19, 18, 17, 16,
+    15, 14, 13, 12, 11, 10, 9, 8, 7, 6, 5, 4, 3, 2, 1, 0,
+)
+REDUCE_ORDER = (
+    19, 6, 9, 20, 24, 22, 27, 1, 10, 28, 3, 13, 2, 5, 18, 25,
+    23, 17, 7, 14, 31, 15, 26, 0, 12, 4, 11, 29, 16, 21, 8, 30,
+)
+
+
 def core_pairs(length):
     return [[chip * CORES + core for core in range(CORES)] for chip in range(length // CORES)]
 
 
-def same_core(length):
-    return [[chip * CORES + core for chip in range(length // CORES)] for core in range(CORES)]
+def same_core(order):
+    return [[chip * CORES + core for chip in order] for core in range(CORES)]
 
 
 def to_partner(x):
@@ -105,9 +115,9 @@
             left_copy(slot).start()
             right_copy(slot).start()
 
-    for chip in range(chips):
+    for place, chip in enumerate(GATHER_ORDER):
         for c in range(CORES):
-            psi_buf[pl.ds((chip * CORES + c) * band, band), :] = psi_ref[c, chip]
+            psi_buf[pl.ds((chip * CORES + c) * band, band), :] = psi_ref[c, place]
     acc_ref[...] = jnp.zeros_like(acc_ref)
 
     def own_term(slot, carry):
@@ -128,9 +138,14 @@
 
     lax.fori_loop(0, own_live, own_term, 0)
     lax.fori_loop(0, partner_live, partner_term, 0)
-    turn = jnp.where(lax.axis_index("sec") == TURNED_SECTOR, chips // 2, 0)
+    turned = lax.axis_index("sec") == TURNED_SECTOR
     for chip in range(chips):
-        sum_ref[lax.rem(chip + turn, chips)] = acc_ref[pl.ds(chip * band, band), :].astype(
+        owner = jnp.where(
+            turned,
+            REDUCE_ORDER.index((chip + chips // 2) % chips),
+            REDUCE_ORDER.index(chip),
+        )
+        sum_ref[owner] = acc_ref[pl.ds(chip * band, band), :].astype(
             jnp.bfloat16
         )
 
@@ -179,10 +194,10 @@
     own_rows = wavefunction[0]
     length, sectors = lax.axis_size("ops"), lax.axis_size("sec")
     chips = length // CORES
-    pairs, peers = core_pairs(length), same_core(length)
+    pairs = core_pairs(length)
 
     copies = jnp.broadcast_to(own_rows[None], (chips, *own_rows.shape))
-    bands = lax.all_to_all(copies, "ops", 0, 0, axis_index_groups=peers, tiled=True)
+    bands = lax.all_to_all(copies, "ops", 0, 0, axis_index_groups=same_core(GATHER_ORDER), tiled=True)
 
     by_band = (left_blocks.shape[1], chips, CORES, own_rows.shape[0], left_blocks.shape[3])
     lefts, rights, meta = fetched_blocks(
@@ -193,7 +208,7 @@
 
     psi = lax.all_gather(bands, "ops", axis_index_groups=pairs)
     chip_sum = summed_terms(psi, meta, lefts, rights, partner_lefts, partner_rights)
-    parts = lax.all_to_all(chip_sum, "ops", 0, 0, axis_index_groups=peers, tiled=True)
+    parts = lax.all_to_all(chip_sum, "ops", 0, 0, axis_index_groups=same_core(REDUCE_ORDER), tiled=True)
     summed = parts.astype(jnp.float32).sum(axis=0)
 
     raised = lax.ppermute(summed, ("ops", "sec"), shift_pairs(length, sectors))

time: 65.2 us -> 64.3 us (0.986)
  blocking collectives: 46.9 us -> 46 us
    all_to_all x2, blocking collectives: 44.7 us -> 43.8 us  [the longest x1 24.4 us: per_device(): lax.all_to_all(copies, 'ops', 0, 0, axis_index_groups=same_core(GATHER_OR...]
where the time goes in v1:
time: 64.3 us; the launch traced here: 64 us
  blocking collectives  46 us (72%)
  starting transfers between devices  8.13 us (13%)
  waiting for transfers between devices  5.4 us (8%)
  local copies, waits for them, and re-layouts  1.98 us (3%)
  Pallas kernels  1.09 us (2%)
  between operations  0.73 us (1%)
  other arithmetic  0.65 us (1%)
    all_to_all x1, blocking collectives, per_device(): lax.all_to_all(copies, 'ops', 0, 0, axis_index_groups=same_core(GATHER_OR...  24.4 us
    all_to_all x1, blocking collectives, per_device(): lax.all_to_all(chip_sum, 'ops', 0, 0, axis_index_groups=same_core(REDUCE_...  19.4 us
    ppermute x1, waiting for transfers between devices, per_device(): raised = lax.ppermute(summed, ('ops', 'sec'), shift_pairs(length, sectors))  5.4 us
    ppermute x2, starting transfers between devices, to_partner(): lax.ppermute(x, 'ops', [(i, i ^ 1) for i in range(lax.axis_size('ops'))])  4.33 us
    ppermute x1, starting transfers between devices, per_device(): raised = lax.ppermute(summed, ('ops', 'sec'), shift_pairs(length, sectors))  3.8 us
    all_gather x1, blocking collectives, per_device(): psi = lax.all_gather(bands, 'ops', axis_index_groups=pairs)  2.17 us
    unnamed x8, local copies, waits for them, and re-layouts  1.96 us
  transfers between devices with their start and end apart: 3, of which 1 were waited for; matrix products, arithmetic and copies ran while one was open for 0% of the time, Pallas kernels for 0%

profile of v1, /device:TPU:56, one launch (start us, length us, event | category | flops | bytes accessed | tf_op | source)
XLA Modules:
  0.0 64.0 jit_solution(12728286105754676605)
XLA Ops:
  0.0 0.0 copy-start
  0.0 0.0 copy-start.3
  0.0 0.9 %fetch.1 = (bf16[4,32,8,512]{3,2,1,0:T(8,128)(2,1)S(1)}, bf16[4,512,512]{2,1,0:T(8,128)(2,1)S(1)}, s32[2]{0:T(128)S(4)}) custom-call(s32[1,64]{1,0:T(1,128)} %counts_ref.1, s32[1,4]{1,0:T(1,128)} %picks_ref.1, bf16[4,32,2,8,512]{4,3,2,1,0:T(8,128)(2,1)} %bitcast.9, bf16[1,4,512,512]{3,2,1,0:T(8,128)(2,1)} %rights_ref.1), custom_call_target="tpu_custom_call" | custom-call | tf_op jit(solution)/shard_map/fetch/pallas_call | solution.py:74
  0.9 1.9 %collective-permute-start.1 = (bf16[4,512,512]{2,1,0:T(8,128)(2,1)S(1)}, bf16[4,512,512]{2,1,0:T(8,128)(2,1)S(1)}, u32[]{:S(2)}, u32[]{:S(2)}) collective-permute-start(bf16[4,512,512]{2,1,0:T(8,128)(2,1)S(1)} %get-tuple-element.10.rights_ref), channel_id=1, source_target_pairs={{0,8},{8,0},{16,24},{24,16},{32,40},{40,32},{48,56},{56,48},{64,72... | collective-permute-start | bytes 6291464 | tf_op jit(solution)/shard_map/ppermute | solution.py:32
  2.9 0.0 copy-done
  2.9 2.4 %collective-permute-start = (bf16[1,4,512,512]{3,2,1,0:T(8,128)(2,1)S(1)}, bf16[1,4,512,512]{3,2,1,0:T(8,128)(2,1)S(1)}, u32[]{:S(2)}, u32[]{:S(2)}) collective-permute-start(bf16[1,4,512,512]{3,2,1,0:T(8,128)(2,1)S(1)} %copy-done), channel_id=1, source_target_pairs={{0,8},{8,0},{16,24},{24,16},{32,40},{40,32},{48,56},{56,48},{64,72... | collective-permute-start | bytes 6291464 | tf_op jit(solution)/shard_map/ppermute | solution.py:32
  5.3 0.0 copy-done.3
  5.3 24.4 %all_to_all.10 = bf16[32,8,512]{2,1,0:T(8,128)(2,1)S(1)} all-to-all(bf16[32,8,512]{2,1,0:T(8,128)(2,1)S(1)} %broadcast_in_dim.8), channel_id=1, replica_groups={{496,480,464,448,432,416,400,384,368,352,336,320,304,288,272,256,240,22..., dimensions={0} | all-to-all | bytes 524288 | tf_op jit(solution)/shard_map/all_to_all | solution.py:200
  29.8 2.2 %all-gather = bf16[64,8,512]{2,1,0:T(8,128)(2,1)S(1)} all-gather(bf16[32,8,512]{2,1,0:T(8,128)(2,1)S(1)} %all_to_all.10), channel_id=2, replica_groups={{0,8},{16,24},{32,40},{48,56},{64,72},{80,88},{96,104},{112,120},{128,1..., dimensions={0}, use_global_device_ids=true | all-gather | bytes 786432 | tf_op jit(solution)/shard_map/all_gather | solution.py:209
  31.9 0.0 collective-permute-done.1.partner_rights_ref
  31.9 0.0 copy-start.1
  31.9 0.0 collective-permute-done
  31.9 0.0 copy-start.2
  31.9 1.3 %copy-done.1 = bf16[4,512,512]{2,1,0:T(8,128)(2,1)} copy-done((bf16[4,512,512]{2,1,0:T(8,128)(2,1)}, bf16[4,512,512]{2,1,0:T(8,128)(2,1)S(1)}, u32[]{:S(2)}) %copy-start.1) | copy-done | bytes 2097176
  33.2 0.7 %copy-done.2 = bf16[1,4,512,512]{3,2,1,0:T(8,128)(2,1)} copy-done((bf16[1,4,512,512]{3,2,1,0:T(8,128)(2,1)}, bf16[1,4,512,512]{3,2,1,0:T(8,128)(2,1)S(1)}, u32[]{:S(2)}) %copy-start.2) | copy-done | bytes 2097176
  33.9 0.2 terms.1
  34.1 19.4 %all_to_all.11 = bf16[32,8,512]{2,1,0:T(8,128)(2,1)S(1)} all-to-all(bf16[32,8,512]{2,1,0:T(8,128)(2,1)S(1)} %terms.1), channel_id=1, replica_groups={{304,96,144,320,384,352,432,16,160,448,48,208,32,80,288,400,368,272,112..., dimensions={0} | all-to-all | bytes 524288 | tf_op jit(solution)/shard_map/all_to_all | solution.py:211
  53.5 3.8 %collective-permute-start.2 = (f32[8,512]{1,0:T(8,128)S(1)}, f32[8,512]{1,0:T(8,128)S(1)}, u32[]{:S(2)}, u32[]{:S(2)}) collective-permute-start(f32[8,512]{1,0:T(8,128)S(1)} %convert_reduce_fusion), channel_id=1, source_target_pairs={{0,1},{1,2},{2,3},{259,4},{4,5},{5,6},{6,7},{8,9},{9,10},{10,11},{... | collective-permute-start | bytes 49160 | tf_op jit(solution)/shard_map/ppermute | solution.py:214
  58.0 5.4 %collective-permute-done.2 = f32[8,512]{1,0:T(8,128)S(1)} collective-permute-done((f32[8,512]{1,0:T(8,128)S(1)}, f32[8,512]{1,0:T(8,128)S(1)}, u32[]{:S(2)}, u32[]{:S(2)}) %collective-permute-start.2) | collective-permute-done | bytes 16416 | tf_op jit(solution)/shard_map/ppermute | solution.py:214
  63.4 0.6 fusion
  (2 shorter events, 0.1 us)
Async XLA Ops:
  0.0 2.9 %copy-start = (bf16[1,4,512,512]{3,2,1,0:T(8,128)(2,1)S(1)}, bf16[1,4,512,512]{3,2,1,0:T(8,128)(2,1)}, u32[]{:S(2)}) copy-start(bf16[1,4,512,512]{3,2,1,0:T(8,128)(2,1)} %param.7) | copy-start | bytes 6291460
  0.0 5.3 %copy-start.3 = (bf16[1,8,512]{2,1,0:T(8,128)(2,1)S(1)}, bf16[1,8,512]{2,1,0:T(8,128)(2,1)}, u32[]{:S(2)}) copy-start(bf16[1,8,512]{2,1,0:T(8,128)(2,1)} %param.6) | copy-start | bytes 24580
  0.9 31.0 %collective-permute-start.1 = (bf16[4,512,512]{2,1,0:T(8,128)(2,1)S(1)}, bf16[4,512,512]{2,1,0:T(8,128)(2,1)S(1)}, u32[]{:S(2)}, u32[]{:S(2)}) collective-permute-start(bf16[4,512,512]{2,1,0:T(8,128)(2,1)S(1)} %get-tuple-element.10.rights_ref), channel_id=1, source_target_pairs={{0,8},{8,0},{16,24},{24,16},{32,40},{40,32},{48,56},{56,48},{64,72... | collective-permute-start | bytes 6291464 | tf_op jit(solution)/shard_map/ppermute | solution.py:32
  2.9 29.1 %collective-permute-start = (bf16[1,4,512,512]{3,2,1,0:T(8,128)(2,1)S(1)}, bf16[1,4,512,512]{3,2,1,0:T(8,128)(2,1)S(1)}, u32[]{:S(2)}, u32[]{:S(2)}) collective-permute-start(bf16[1,4,512,512]{3,2,1,0:T(8,128)(2,1)S(1)} %copy-done), channel_id=1, source_target_pairs={{0,8},{8,0},{16,24},{24,16},{32,40},{40,32},{48,56},{56,48},{64,72... | collective-permute-start | bytes 6291464 | tf_op jit(solution)/shard_map/ppermute | solution.py:32
  31.9 1.3 %copy-start.1 = (bf16[4,512,512]{2,1,0:T(8,128)(2,1)}, bf16[4,512,512]{2,1,0:T(8,128)(2,1)S(1)}, u32[]{:S(2)}) copy-start(bf16[4,512,512]{2,1,0:T(8,128)(2,1)S(1)} %collective-permute-done.1.partner_rights_ref) | copy-start | bytes 6291460
  31.9 2.0 %copy-start.2 = (bf16[1,4,512,512]{3,2,1,0:T(8,128)(2,1)}, bf16[1,4,512,512]{3,2,1,0:T(8,128)(2,1)S(1)}, u32[]{:S(2)}) copy-start(bf16[1,4,512,512]{3,2,1,0:T(8,128)(2,1)S(1)} %collective-permute-done) | copy-start | bytes 6291460
  53.5 9.9 %collective-permute-start.2 = (f32[8,512]{1,0:T(8,128)S(1)}, f32[8,512]{1,0:T(8,128)S(1)}, u32[]{:S(2)}, u32[]{:S(2)}) collective-permute-start(f32[8,512]{1,0:T(8,128)S(1)} %convert_reduce_fusion), channel_id=1, source_target_pairs={{0,1},{1,2},{2,3},{259,4},{4,5},{5,6},{6,7},{8,9},{9,10},{10,11},{... | collective-permute-start | bytes 49160 | tf_op jit(solution)/shard_map/ppermute | solution.py:214

commit v2 on v1

--- a/solution.py
+++ b/solution.py
@@ -7,6 +7,7 @@
 
 
 CORES = 2
+PIECES = 4
 TURNED_SECTOR = 3
 
 
@@ -112,8 +113,20 @@
 
         @pl.when(slot < partner_live)
         def _():
-            left_copy(slot).start()
-            right_copy(slot).start()
+            for piece in range(PIECES):
+                part = pl.ds(piece * (chips // PIECES), chips // PIECES)
+                pltpu.make_async_copy(
+                    partner_lefts_ref.at[slot, part, core],
+                    left_buf.at[slot, part],
+                    left_sems.at[slot],
+                ).start()
+            for piece in range(PIECES):
+                part = pl.ds(piece * (size // PIECES), size // PIECES)
+                pltpu.make_async_copy(
+                    partner_rights_ref.at[slot, part],
+                    right_buf.at[slot, part],
+                    right_sems.at[slot],
+                ).start()
 
     for place, chip in enumerate(GATHER_ORDER):
         for c in range(CORES):

time: 64.3 us -> 64.3 us (level)
  no operation moved by 1% of the time
where the time goes in v2:
time: 64.3 us; the launch traced here: 64 us
  blocking collectives  46 us (72%)
  starting transfers between devices  7.98 us (12%)
  waiting for transfers between devices  5.55 us (9%)
  local copies, waits for them, and re-layouts  1.98 us (3%)
  Pallas kernels  1.1 us (2%)
  between operations  0.73 us (1%)
  other arithmetic  0.65 us (1%)
    all_to_all x1, blocking collectives, per_device(): lax.all_to_all(copies, 'ops', 0, 0, axis_index_groups=same_core(GATHER_OR...  24.4 us
    all_to_all x1, blocking collectives, per_device(): lax.all_to_all(chip_sum, 'ops', 0, 0, axis_index_groups=same_core(REDUCE_...  19.4 us
    ppermute x1, waiting for transfers between devices, per_device(): raised = lax.ppermute(summed, ('ops', 'sec'), shift_pairs(length, sectors))  5.54 us
    ppermute x2, starting transfers between devices, to_partner(): lax.ppermute(x, 'ops', [(i, i ^ 1) for i in range(lax.axis_size('ops'))])  4.33 us
    ppermute x1, starting transfers between devices, per_device(): raised = lax.ppermute(summed, ('ops', 'sec'), shift_pairs(length, sectors))  3.65 us
    all_gather x1, blocking collectives, per_device(): psi = lax.all_gather(bands, 'ops', axis_index_groups=pairs)  2.17 us
    unnamed x8, local copies, waits for them, and re-layouts  1.96 us
  transfers between devices with their start and end apart: 3, of which 1 were waited for; matrix products, arithmetic and copies ran while one was open for 0% of the time, Pallas kernels for 0%

profile of v2, /device:TPU:56, one launch (start us, length us, event | category | flops | bytes accessed | tf_op | source)
XLA Modules:
  0.0 64.0 jit_solution(5015933240128114391)
XLA Ops:
  0.0 0.0 copy-start
  0.0 0.0 copy-start.3
  0.0 0.9 %fetch.1 = (bf16[4,32,8,512]{3,2,1,0:T(8,128)(2,1)S(1)}, bf16[4,512,512]{2,1,0:T(8,128)(2,1)S(1)}, s32[2]{0:T(128)S(4)}) custom-call(s32[1,64]{1,0:T(1,128)} %counts_ref.1, s32[1,4]{1,0:T(1,128)} %picks_ref.1, bf16[4,32,2,8,512]{4,3,2,1,0:T(8,128)(2,1)} %bitcast.9, bf16[1,4,512,512]{3,2,1,0:T(8,128)(2,1)} %rights_ref.1), custom_call_target="tpu_custom_call" | custom-call | tf_op jit(solution)/shard_map/fetch/pallas_call | solution.py:75
  0.9 1.9 %collective-permute-start.1 = (bf16[4,512,512]{2,1,0:T(8,128)(2,1)S(1)}, bf16[4,512,512]{2,1,0:T(8,128)(2,1)S(1)}, u32[]{:S(2)}, u32[]{:S(2)}) collective-permute-start(bf16[4,512,512]{2,1,0:T(8,128)(2,1)S(1)} %get-tuple-element.10.rights_ref), channel_id=1, source_target_pairs={{0,8},{8,0},{16,24},{24,16},{32,40},{40,32},{48,56},{56,48},{64,72... | collective-permute-start | bytes 6291464 | tf_op jit(solution)/shard_map/ppermute | solution.py:33
  2.9 0.0 copy-done
  2.9 2.4 %collective-permute-start = (bf16[1,4,512,512]{3,2,1,0:T(8,128)(2,1)S(1)}, bf16[1,4,512,512]{3,2,1,0:T(8,128)(2,1)S(1)}, u32[]{:S(2)}, u32[]{:S(2)}) collective-permute-start(bf16[1,4,512,512]{3,2,1,0:T(8,128)(2,1)S(1)} %copy-done), channel_id=1, source_target_pairs={{0,8},{8,0},{16,24},{24,16},{32,40},{40,32},{48,56},{56,48},{64,72... | collective-permute-start | bytes 6291464 | tf_op jit(solution)/shard_map/ppermute | solution.py:33
  5.3 0.0 copy-done.3
  5.3 24.4 %all_to_all.10 = bf16[32,8,512]{2,1,0:T(8,128)(2,1)S(1)} all-to-all(bf16[32,8,512]{2,1,0:T(8,128)(2,1)S(1)} %broadcast_in_dim.8), channel_id=1, replica_groups={{496,480,464,448,432,416,400,384,368,352,336,320,304,288,272,256,240,22..., dimensions={0} | all-to-all | bytes 524288 | tf_op jit(solution)/shard_map/all_to_all | solution.py:213
  29.8 2.2 %all-gather = bf16[64,8,512]{2,1,0:T(8,128)(2,1)S(1)} all-gather(bf16[32,8,512]{2,1,0:T(8,128)(2,1)S(1)} %all_to_all.10), channel_id=2, replica_groups={{0,8},{16,24},{32,40},{48,56},{64,72},{80,88},{96,104},{112,120},{128,1..., dimensions={0}, use_global_device_ids=true | all-gather | bytes 786432 | tf_op jit(solution)/shard_map/all_gather | solution.py:222
  31.9 0.0 collective-permute-done.1.partner_rights_ref
  31.9 0.0 copy-start.1
  31.9 0.0 collective-permute-done
  31.9 0.0 copy-start.2
  31.9 1.3 %copy-done.1 = bf16[4,512,512]{2,1,0:T(8,128)(2,1)} copy-done((bf16[4,512,512]{2,1,0:T(8,128)(2,1)}, bf16[4,512,512]{2,1,0:T(8,128)(2,1)S(1)}, u32[]{:S(2)}) %copy-start.1) | copy-done | bytes 2097176
  33.2 0.7 %copy-done.2 = bf16[1,4,512,512]{3,2,1,0:T(8,128)(2,1)} copy-done((bf16[1,4,512,512]{3,2,1,0:T(8,128)(2,1)}, bf16[1,4,512,512]{3,2,1,0:T(8,128)(2,1)S(1)}, u32[]{:S(2)}) %copy-start.2) | copy-done | bytes 2097176
  33.9 0.2 terms.1
  34.1 19.4 %all_to_all.11 = bf16[32,8,512]{2,1,0:T(8,128)(2,1)S(1)} all-to-all(bf16[32,8,512]{2,1,0:T(8,128)(2,1)S(1)} %terms.1), channel_id=1, replica_groups={{304,96,144,320,384,352,432,16,160,448,48,208,32,80,288,400,368,272,112..., dimensions={0} | all-to-all | bytes 524288 | tf_op jit(solution)/shard_map/all_to_all | solution.py:224
  53.5 3.7 %collective-permute-start.2 = (f32[8,512]{1,0:T(8,128)S(1)}, f32[8,512]{1,0:T(8,128)S(1)}, u32[]{:S(2)}, u32[]{:S(2)}) collective-permute-start(f32[8,512]{1,0:T(8,128)S(1)} %convert_reduce_fusion), channel_id=1, source_target_pairs={{0,1},{1,2},{2,3},{259,4},{4,5},{5,6},{6,7},{8,9},{9,10},{10,11},{... | collective-permute-start | bytes 49160 | tf_op jit(solution)/shard_map/ppermute | solution.py:227
  57.8 5.5 %collective-permute-done.2 = f32[8,512]{1,0:T(8,128)S(1)} collective-permute-done((f32[8,512]{1,0:T(8,128)S(1)}, f32[8,512]{1,0:T(8,128)S(1)}, u32[]{:S(2)}, u32[]{:S(2)}) %collective-permute-start.2) | collective-permute-done | bytes 16416 | tf_op jit(solution)/shard_map/ppermute | solution.py:227
  63.4 0.6 fusion
  (2 shorter events, 0.1 us)
Async XLA Ops:
  0.0 2.9 %copy-start = (bf16[1,4,512,512]{3,2,1,0:T(8,128)(2,1)S(1)}, bf16[1,4,512,512]{3,2,1,0:T(8,128)(2,1)}, u32[]{:S(2)}) copy-start(bf16[1,4,512,512]{3,2,1,0:T(8,128)(2,1)} %param.7) | copy-start | bytes 6291460
  0.0 5.3 %copy-start.3 = (bf16[1,8,512]{2,1,0:T(8,128)(2,1)S(1)}, bf16[1,8,512]{2,1,0:T(8,128)(2,1)}, u32[]{:S(2)}) copy-start(bf16[1,8,512]{2,1,0:T(8,128)(2,1)} %param.6) | copy-start | bytes 24580
  0.9 31.0 %collective-permute-start.1 = (bf16[4,512,512]{2,1,0:T(8,128)(2,1)S(1)}, bf16[4,512,512]{2,1,0:T(8,128)(2,1)S(1)}, u32[]{:S(2)}, u32[]{:S(2)}) collective-permute-start(bf16[4,512,512]{2,1,0:T(8,128)(2,1)S(1)} %get-tuple-element.10.rights_ref), channel_id=1, source_target_pairs={{0,8},{8,0},{16,24},{24,16},{32,40},{40,32},{48,56},{56,48},{64,72... | collective-permute-start | bytes 6291464 | tf_op jit(solution)/shard_map/ppermute | solution.py:33
  2.9 29.1 %collective-permute-start = (bf16[1,4,512,512]{3,2,1,0:T(8,128)(2,1)S(1)}, bf16[1,4,512,512]{3,2,1,0:T(8,128)(2,1)S(1)}, u32[]{:S(2)}, u32[]{:S(2)}) collective-permute-start(bf16[1,4,512,512]{3,2,1,0:T(8,128)(2,1)S(1)} %copy-done), channel_id=1, source_target_pairs={{0,8},{8,0},{16,24},{24,16},{32,40},{40,32},{48,56},{56,48},{64,72... | collective-permute-start | bytes 6291464 | tf_op jit(solution)/shard_map/ppermute | solution.py:33
  31.9 1.3 %copy-start.1 = (bf16[4,512,512]{2,1,0:T(8,128)(2,1)}, bf16[4,512,512]{2,1,0:T(8,128)(2,1)S(1)}, u32[]{:S(2)}) copy-start(bf16[4,512,512]{2,1,0:T(8,128)(2,1)S(1)} %collective-permute-done.1.partner_rights_ref) | copy-start | bytes 6291460
  31.9 2.0 %copy-start.2 = (bf16[1,4,512,512]{3,2,1,0:T(8,128)(2,1)}, bf16[1,4,512,512]{3,2,1,0:T(8,128)(2,1)S(1)}, u32[]{:S(2)}) copy-start(bf16[1,4,512,512]{3,2,1,0:T(8,128)(2,1)S(1)} %collective-permute-done) | copy-start | bytes 6291460
  53.5 9.9 %collective-permute-start.2 = (f32[8,512]{1,0:T(8,128)S(1)}, f32[8,512]{1,0:T(8,128)S(1)}, u32[]{:S(2)}, u32[]{:S(2)}) collective-permute-start(f32[8,512]{1,0:T(8,128)S(1)} %convert_reduce_fusion), channel_id=1, source_target_pairs={{0,1},{1,2},{2,3},{259,4},{4,5},{5,6},{6,7},{8,9},{9,10},{10,11},{... | collective-permute-start | bytes 49160 | tf_op jit(solution)/shard_map/ppermute | solution.py:227
